TPU v7x, 32 devices: a whole 2x2x4 slice. The times are simulated.
32 devices in a mesh: row: 16 (over z, y, x), width: 2 (over core).
Axes of the slice: x: 2, y: 2, z: 4, core: 2. Of those that a mesh axis runs over, the one named last changes fastest.
Arguments:
- row_numbers: int32 [512, 2], P('row'), may hold values from 0 to 16383
- item_table: bfloat16 [16384, 64], P('row', 'width'), may hold values from -6 to 6
- dense_part: float32 [512, 64], P('row', 'width'), may hold values from -6 to 6
- small_ids: int32 [512], P('row'), may hold values from 0 to 31
- small_table: bfloat16 [32, 64], P('row', 'width'), may hold values from -6 to 6
Outputs:
- features: bfloat16 [512, 3, 64], P('row', None, 'width')
All inputs are finite; a program needn't handle non-finite values.
Results may differ from a plain program's by a relative error of at most 0.0004.
Values may be sent and summed in bfloat16 or wider, within the bound.
A program may use at most 64 MiB of HBM per device.

v0:
```python
import jax
import jax.numpy as jnp
from jax import lax
from jax.sharding import PartitionSpec as P

PICKS = 2


def summed_rows(product, span, axis):
    everything = product(jnp.int32(0), lax.axis_size(axis) * span)
    own = lax.psum_scatter(everything, axis, scatter_dimension=0, tiled=True)
    return own


def own_rows(table_part, wanted, first_row):
    place = wanted - first_row
    inside = (place >= 0) & (place < table_part.shape[0])
    found = jnp.take(table_part, jnp.clip(place, 0, table_part.shape[0] - 1), axis=0).astype(
        jnp.float32
    )
    return jnp.where(inside[..., None], found, 0.0)


def per_device(row_numbers, item_table, dense_part, small_ids, small_table):
    big_first = lax.axis_index("row") * item_table.shape[0]
    all_ids = lax.all_gather(row_numbers, "row", axis=0, tiled=True)

    def pooled_part(start, count):
        wanted = lax.dynamic_slice_in_dim(all_ids, start, count)
        return jnp.sum(own_rows(item_table, wanted, big_first), axis=1)

    pooled = summed_rows(pooled_part, row_numbers.shape[0], "row") * PICKS ** (-0.5)
    every_row = lax.all_gather(small_table, "row", axis=0, tiled=True)
    small_rows = jnp.take(every_row, small_ids, axis=0).astype(jnp.float32)
    features = jnp.stack([dense_part, pooled, small_rows], axis=1).astype(jnp.bfloat16)
    return features


def solution(mesh):
    placed = (P("row", None), P("row", "width"), P("row", "width"), P("row"), P("row", "width"))
    return jax.shard_map(
        per_device, mesh=mesh, in_specs=placed, out_specs=P("row", None, "width"), check_vma=False
    )
```

profile of v0, /device:TPU:0, one launch (start us, length us, event | category | flops | bytes accessed | tf_op | source)
XLA Modules:
  0.0 139.5 jit_solution(6048867107979363630)
XLA Ops:
  6.5 0.0 reduce-scatter.2.cloned.1.call-start
  6.5 0.0 copy-start.2
  6.5 0.7 copy-done.2
  7.2 42.5 %all-gather = s32[16,32,2]{1,2,0:T(2,128)S(1)} all-gather(s32[1,32,2]{1,2,0:T(2,128)S(1)} %bitcast.16), channel_id=1, replica_groups=mesh['row'=16,'width'=2] {'row'}, dimensions={0}, use_global_device_ids=true | all-gather | bytes 4352 | tf_op jit(solution)/shard_map/all_gather | solution.py:26
  49.7 0.1 reshape.69
  49.9 0.1 copy.22
  50.0 0.0 copy-start
  50.0 0.2 reshape.40
  50.2 0.7 copy-done
  50.9 0.2 copy.23
  51.1 0.2 copy.21
  51.3 0.2 copy.24
  51.5 3.2 %gather_fusion = bf16[1024,32]{1,0:T(8,128)(2,1)S(1)} fusion(bf16[1024,32]{1,0:T(8,128)(2,1)S(1)} %copy.23, s32[1024]{0:T(1024)S(1)} %broadcast_clamp_fusion), kind=kCustom, calls=%fused_computation | custom fusion | bytes 135168 | tf_op jit(solution)/shard_map/jit(_take)/gather | solution.py:18
  54.7 3.6 %select_reduce_fusion = f32[512,32]{1,0:T(8,128)} fusion(pred[512,2]{1,0:T(8,128)(4,1)S(1)} %bitcast.15, bf16[512,2,32]{2,1,0:T(2,128)(2,1)S(1)} %bitcast.13, pred[512,2]{1,0:T(8,128)(4,1)S(1)} %copy.21), kind=kLoop, calls=%fused_computation.2 | loop fusion | flops 114688 | bytes 133120 | tf_op jit(solution)/shard_map/reduce_sum | solution.py:30
  58.3 0.0 copy-start.4
  58.3 0.0 copy-start.3
  58.3 0.0 reduce-scatter.2.cloned.1.call-update
  58.3 0.6 copy-done.4
  58.9 0.0 copy-start.1
  58.9 0.0 copy-done.3
  58.9 35.6 %all-gather.1 = bf16[16,2,32]{2,1,0:T(2,128)(2,1)S(1)} all-gather(bf16[1,2,32]{2,1,0:T(2,128)(2,1)S(1)} %bitcast.17), channel_id=1, replica_groups=mesh['row'=16,'width'=2] {'row'}, dimensions={0}, use_global_device_ids=true | all-gather | bytes 2176 | tf_op jit(solution)/shard_map/all_gather | solution.py:33
  94.5 0.0 copy-done.1
  94.5 0.6 gather_fusion.1
  95.1 0.1 bitcast_select_fusion
  95.2 36.2 %reduce-scatter.2.cloned.1.call-done = f32[32,32]{1,0:T(8,128)} async-done(((f32[512,32]{1,0:T(8,128)}), f32[32,32]{1,0:T(8,128)}) %reduce-scatter.2.cloned.1.call-update) | async-done | bytes 4112 | tf_op jit(solution)/shard_map/reduce_scatter | solution.py:11
  131.4 0.7 fusion.1
  132.1 0.6 pad_maximum_fusion
  (9 shorter events, 0.1 us)
Async XLA Ops:
  6.5 124.8 %reduce-scatter.2.cloned.1.call-start = ((), (), s32[]{:S(2)}) async-start(), calls=%async_computation.1 | async-start | bytes 278528 | tf_op jit(solution)/shard_map/reduce_scatter | solution.py:11
  6.5 0.7 copy-start.2
  50.0 0.8 copy-start
  58.3 0.7 copy-start.4
  58.3 0.7 copy-start.3
  58.9 35.6 %copy-start.1 = (f32[32,32]{1,0:T(8,128)S(1)}, f32[32,32]{1,0:T(8,128)}, u32[]{:S(2)}) copy-start(f32[32,32]{1,0:T(8,128)} %param.7) | copy-start | bytes 12292
Sparse Core Ops, SparseCore 0:
  58.4 72.9 reduce-scatter.1
where the time goes:
time: 140 us
  blocking collectives  78.1 us (56%)
  waiting for transfers between devices  36.2 us (26%)
  between operations  13.5 us (10%)
  local copies, waits for them, and re-layouts  6.76 us (5%)
  other arithmetic  5.05 us (4%)
    all_gather x1, blocking collectives, per_device(): all_ids = lax.all_gather(row_numbers, 'row', axis=0, tiled=True)  42.5 us
    reduce_scatter x1, waiting for transfers between devices, summed_rows(): own = lax.psum_scatter(everything, axis, scatter_dimension=0, tiled=True)  36.2 us
    all_gather x1, blocking collectives, per_device(): every_row = lax.all_gather(small_table, 'row', axis=0, tiled=True)  35.6 us
    reduce_sum x1, other arithmetic, pooled_part(): return jnp.sum(own_rows(item_table, wanted, big_first), axis=1)  3.58 us
    gather x1, local copies, waits for them, and re-layouts, own_rows(): jnp.take(table_part, jnp.clip(place, 0, table_part.shape[0] - 1), axis=0)  3.2 us
  transfers between devices with their start and end apart: 1, of which 1 were waited for; matrix products, arithmetic and copies ran while one was open for 0% of the time, Pallas kernels for 0%

commit v1 on v0

v1 whole, which is shorter than its diff:
```python
import functools

import jax
import jax.numpy as jnp
from jax import lax
from jax.experimental import pallas as pl
from jax.experimental.pallas import tpu as pltpu
from jax.sharding import PartitionSpec as P

MESH = pl.DeviceIdType.MESH


def near_size(count):
    return max(d for d in range(1, count + 1) if count % d == 0 and d * d <= count)


def target(place, step, count):
    return place ^ step if count & (count - 1) == 0 else (place + step) % count


def source(place, step, count):
    return place ^ step if count & (count - 1) == 0 else (place - step + count) % count


def kernel(
    near, far, scale,
    ids_hbm, table_hbm, dense_hbm, small_ids_hbm, small_hbm, out_ref,
    ids, tables, dense, small_ids, smalls, packed, arrived,
    local_sem, ids_out, ids_in, tab_out, tab_in, sm_out, sm_in, sf_out, sf_in, val_out, val_in,
):
    me = lax.axis_index("row")
    low, high = me % near, me // near
    picks, examples = ids.shape[1:]
    features, rows = tables.shape[1:]
    small_span = smalls.shape[2]

    def near_to(step):
        return {"row": high * near + target(low, step, near)}

    def far_to(step):
        return {"row": target(high, step, far) * near + low}

    def far_back(step):
        return {"row": source(high, step, far) * near + low}

    barrier = pltpu.get_barrier_semaphore()
    for step in range(1, far):
        pl.semaphore_signal(barrier, inc=1, device_id=far_to(step), device_id_type=MESH)
    for step in range(1, near):
        pl.semaphore_signal(barrier, inc=1, device_id=near_to(step), device_id_type=MESH)

    own = [
        pltpu.make_async_copy(src, dst, local_sem.at[i])
        for i, (src, dst) in enumerate(
            [
                (ids_hbm, ids.at[0]),
                (table_hbm, tables.at[0]),
                (small_hbm, smalls.at[0, 0]),
                (dense_hbm, dense),
                (small_ids_hbm, small_ids),
            ]
        )
    ]
    for copy in own:
        copy.start()

    def remote(src, dst, out_sem, in_sem, device):
        return pltpu.make_async_remote_copy(
            src_ref=src, dst_ref=dst, send_sem=out_sem, recv_sem=in_sem,
            device_id=device, device_id_type=MESH,
        )

    ids_copies = [
        remote(ids.at[0], ids.at[s], ids_out.at[s], ids_in.at[s], far_to(s)) for s in range(1, far)
    ]
    table_copies = [
        remote(tables.at[0], tables.at[s], tab_out.at[s], tab_in.at[s], near_to(s))
        for s in range(1, near)
    ]
    small_copies = [
        remote(smalls.at[0, 0], smalls.at[0, s], sm_out.at[s], sm_in.at[s], near_to(s))
        for s in range(1, near)
    ]
    small_far = [
        remote(smalls.at[0], smalls.at[s], sf_out.at[s], sf_in.at[s], far_to(s))
        for s in range(1, far)
    ]
    value_copies = [
        remote(packed.at[s], arrived.at[s], val_out.at[s], val_in.at[s], far_back(s))
        for s in range(1, far)
    ]

    own[0].wait()
    own[1].wait()
    own[2].wait()
    pl.semaphore_wait(barrier, far - 1 + near - 1)
    for copy in reversed(ids_copies):
        copy.start()
    for copy in small_copies:
        copy.start()
    for copy in reversed(table_copies):
        copy.start()

    own[3].wait()
    own[4].wait()
    out_ref[0] = dense[...].astype(out_ref.dtype)

    for copy in ids_copies:
        copy.wait_recv()
    wanted = jnp.concatenate([ids[s] for s in range(far)], axis=1)
    lanes = far * examples
    spot = lax.broadcasted_iota(jnp.int32, (rows, lanes), 0)

    def chosen(step):
        first = (high * near + source(low, step, near)) * rows
        hits = 0.0
        for pick in range(picks):
            hits = hits + jnp.where(spot == wanted[pick : pick + 1] - first, 1.0, 0.0)
        return hits.astype(tables.dtype)

    found = jnp.zeros((features, lanes), jnp.float32)
    for step in range(near):
        hits = chosen(step)
        if step:
            small_copies[step - 1].wait_recv()
            table_copies[step - 1].wait_recv()
        found = found + jnp.dot(tables[step], hits, preferred_element_type=jnp.float32)

    blocks = features // 8
    for step in reversed(range(far)):
        packed[step] = jnp.concatenate(
            [
                found[8 * b : 8 * b + 8, step * examples : (step + 1) * examples]
                for b in range(blocks)
            ],
            axis=1,
        )
        if step:
            value_copies[step - 1].start()
    for copy in reversed(small_far):
        copy.start()

    small_column = jnp.broadcast_to(small_ids[...], (8, examples)).T[:, 0:1]
    for copy in small_far:
        copy.wait_recv()
    rows_out = jnp.zeros((examples, features), jnp.float32)
    for far_step in range(far):
        for near_step in range(near):
            device = source(high, far_step, far) * near + source(low, near_step, near)
            part = smalls[far_step, near_step].astype(jnp.float32)
            for r in range(small_span):
                rows_out = jnp.where(
                    small_column == device * small_span + r, part[r : r + 1], rows_out
                )
    out_ref[2] = rows_out.astype(out_ref.dtype)

    total = packed[0]
    for step in range(1, far):
        value_copies[step - 1].wait_recv()
        total = total + arrived[step]
    total = total * scale
    pooled = jnp.concatenate(
        [total[:, b * examples : (b + 1) * examples] for b in range(blocks)], axis=0
    ).T
    out_ref[1] = pooled.astype(out_ref.dtype)

    for copy in ids_copies + table_copies + small_copies + small_far + value_copies:
        copy.wait_send()


def per_device(count, row_numbers, item_table, dense_part, small_ids, small_table):
    near = near_size(count)
    far = count // near
    examples, picks = row_numbers.shape
    rows, features = item_table.shape
    dma = pltpu.SemaphoreType.DMA
    out = pl.pallas_call(
        functools.partial(kernel, near, far, picks ** (-0.5)),
        out_shape=jax.ShapeDtypeStruct((3, examples, features), jnp.bfloat16),
        in_specs=[pl.BlockSpec(memory_space=pl.ANY)] * 5,
        out_specs=pl.BlockSpec(memory_space=pltpu.VMEM),
        scratch_shapes=[
            pltpu.VMEM((far, picks, examples), jnp.int32),
            pltpu.VMEM((near, features, rows), item_table.dtype),
            pltpu.VMEM(dense_part.shape, dense_part.dtype),
            pltpu.VMEM((1, examples), jnp.int32),
            pltpu.VMEM((far, near) + small_table.shape, small_table.dtype),
            pltpu.VMEM((far, 8, features // 8 * examples), jnp.float32),
            pltpu.VMEM((far, 8, features // 8 * examples), jnp.float32),
            dma((5,)),
            dma((far,)), dma((far,)),
            dma((near,)), dma((near,)),
            dma((near,)), dma((near,)),
            dma((far,)), dma((far,)),
            dma((far,)), dma((far,)),
        ],
        compiler_params=pltpu.CompilerParams(collective_id=0, has_side_effects=True),
    )(row_numbers.T, item_table.T, dense_part, small_ids[None, :], small_table)
    return jnp.transpose(out, (1, 0, 2))


def solution(mesh):
    placed = (P("row", None), P("row", "width"), P("row", "width"), P("row"), P("row", "width"))
    return jax.shard_map(
        functools.partial(per_device, mesh.shape["row"]),
        mesh=mesh, in_specs=placed, out_specs=P("row", None, "width"), check_vma=False,
    )
```

time: 140 us -> 16.9 us (0.12)
  blocking collectives: 78.1 us -> 0 us
  waiting for transfers between devices: 36.2 us -> 0 us
  Pallas kernels: 0 us -> 15.3 us
  between operations: 13.5 us -> 0.01 us
  local copies, waits for them, and re-layouts: 6.76 us -> 1.35 us
  other arithmetic: 5.05 us -> 0 us
    all_gather x2 -> x0, blocking collectives: 78.1 us -> none  [the longest x1 42.5 us: per_device(): all_ids = lax.all_gather(row_numbers, 'row', axis=0, tiled=True)]
    reduce_scatter x1 -> x0, waiting for transfers between devices: 36.2 us -> none  [summed_rows(): own = lax.psum_scatter(everything, axis, scatter_dimension=0, tiled=True)]
    pallas_call x0 -> x1, Pallas kernels: none -> 15.3 us  [per_device(): pl.pallas_call(functools.partial(kernel, near, far, picks ** (-0.5)), out...]
    gather x2 -> x0, local copies, waits for them, and re-layouts: 3.8 us -> none  [the longest x1 3.2 us: own_rows(): jnp.take(table_part, jnp.clip(place, 0, table_part.shape[0] - 1), axis=0)]
    reduce_sum x1 -> x0, other arithmetic: 3.58 us -> none  [pooled_part(): return jnp.sum(own_rows(item_table, wanted, big_first), axis=1)]
  transfers between devices with their start and end apart: 1 -> 0, of which waited for: 1 -> 0; matrix products, arithmetic and copies ran while one was open for 0% -> 0% of each run, Pallas kernels for 0% -> 0%
where the time goes in v1:
time: 16.9 us; the launch traced here: 16.7 us
  Pallas kernels  15.3 us (91%)
  local copies, waits for them, and re-layouts  1.35 us (8%)
    pallas_call x1, Pallas kernels, per_device(): pl.pallas_call(functools.partial(kernel, near, far, picks ** (-0.5)), out...  15.3 us
    unnamed x1, local copies, waits for them, and re-layouts  1.35 us

profile of v1, /device:TPU:0, one launch (start us, length us, event | category | flops | bytes accessed | tf_op | source)
XLA Modules:
  0.0 16.7 jit_solution(13634352406948790972)
XLA Ops:
  0.0 15.3 %shard_map.55 = bf16[3,32,32]{2,1,0:T(8,128)(2,1)} custom-call(s32[2,32]{1,0:T(2,128)} %bitcast.6, bf16[32,1024]{1,0:T(8,128)(2,1)} %bitcast.5, f32[32,32]{1,0:T(8,128)} %dense_hbm.1, s32[1,32]{1,0:T(1,128)} %bitcast.7, bf16[2,32]{1,0:T(2,128)(2,1)} %small_hbm.1), custom_call_target="tpu_custom_call" | custom-call | tf_op jit(solution)/shard_map/pallas_call | solution.py:177
  15.3 1.3 %copy.7 = bf16[32,3,32]{2,0,1:T(8,128)(2,1)} copy(bf16[32,3,32]{2,0,1:T(8,128)(2,1)} %bitcast.4) | data formatting | bytes 12288
